TPU v7x, 256 devices: a whole 4x4x8 slice. The times are simulated.
256 devices in a mesh: row: 32 (over y, z), col: 8 (over x, core).
Axes of the slice: x: 4, y: 4, z: 8, core: 2. Of those that a mesh axis runs over, the one named last changes fastest.
Arguments:
- grams: bfloat16 [4, 3584, 3584], P(None, 'row', 'col'), as said below
- weights: bfloat16 [4, 3584, 7168], P(None, 'row', 'col'), may hold values from -6 to 6
Outputs:
- merged: float32 [3584, 7168], P('row', 'col')
- residual: float32 [3584, 7168], P('row', 'col')
Inputs may be any that keep to these rules, and one draw needn't show every extreme that they name: `grams`: each of the 4 matrices is symmetric and positive definite.
All inputs are finite; a program needn't handle non-finite values.
Results may differ from a plain program's by a relative error of at most 0.012.
The roundings to bfloat16 on the way count: a program that leaves them out, or rounds other values in their place, can miss the bound.
Values may be sent and summed in bfloat16 or wider, within the bound.
A program may use at most 256 MiB of HBM per device.

v0:
```python
import jax
import jax.numpy as jnp
from jax import lax
from jax.sharding import Mesh
from jax.sharding import PartitionSpec as P

ITERS = 2
ROW = ("row_0", "row_1")


def sum_by_axis(so_far, axes):
    for axis in axes:
        so_far = lax.psum_scatter(so_far, axis, scatter_dimension=0, tiled=True)
    return so_far


def sent_to_all(x, axis):
    copies = jnp.broadcast_to(x, (lax.axis_size(axis), *x.shape))
    return lax.all_to_all(copies, axis, split_axis=0, concat_axis=0, tiled=True)


def of_everyone(x, axis):
    return sent_to_all(x, axis).sum(axis=0)


def together(arrays, axis):
    ravelled, at, done = (jnp.concatenate([a.reshape(-1) for a in arrays]), 0, [])
    so_far = of_everyone(ravelled, axis)
    for a in arrays:
        done.append(so_far[at : at + a.size].reshape(a.shape))
        at += a.size
    return tuple(done)


def shards(grams, weights):
    slab_rows = grams.shape[1]
    col_count = weights.shape[2]
    first_row = lax.axis_index(ROW) * slab_rows
    high = lax.Precision.HIGHEST
    gram_slabs = lax.all_gather(grams, "col", axis=2, tiled=True)
    gram_total = jnp.sum(gram_slabs, axis=0, dtype=jnp.float32)
    square_block = lax.dynamic_slice_in_dim(gram_slabs, first_row, slab_rows, gram_slabs.ndim - 1)
    diag_total = jnp.einsum(
        "mr,mrc->rc",
        jnp.diagonal(square_block, axis1=-2, axis2=-1).astype(jnp.float32),
        weights.astype(jnp.float32),
    )
    product = sum_by_axis(
        jnp.einsum("mrk,mrc->kc", gram_slabs, weights, preferred_element_type=jnp.float32), ROW
    )
    right_side = 0.9 * product + 0.1 * diag_total
    total_diag = jnp.diagonal(lax.dynamic_slice_in_dim(gram_total, first_row, slab_rows, 1))
    merged = jnp.zeros((slab_rows, col_count), jnp.float32)
    residual = right_side
    direction = right_side
    for iteration in range(ITERS):
        rounded = direction.astype(jnp.bfloat16)
        shard_piece = lax.all_gather(rounded, ROW, axis=0, tiled=True)
        add_columns = lax.slice_in_dim(gram_total, 0, shard_piece.shape[0], axis=1)
        mapped = jnp.zeros((slab_rows, col_count), jnp.float32) + jnp.dot(
            add_columns, shard_piece.astype(jnp.float32), precision=high
        )
        mapped = 0.9 * mapped + 0.1 * total_diag[:, None] * rounded.astype(jnp.float32)
        curvature, cross_term, square, norm_now = together(
            (
                jnp.sum(direction * mapped, axis=0),
                jnp.sum(residual * mapped, axis=0),
                jnp.sum(mapped * mapped, axis=0),
                jnp.sum(residual * residual, axis=0),
            ),
            ROW,
        )
        step_length = norm_now / curvature
        merged = merged + step_length * direction
        residual = residual - step_length * mapped
        if iteration + 1 < ITERS:
            norm_next = (
                norm_now - 2.0 * step_length * cross_term + step_length * step_length * square
            )
            direction = residual + norm_next / norm_now * direction
    return (merged, residual)


def solution(mesh):
    torus = Mesh(mesh.devices.reshape(4, 8, mesh.shape["col"]), ("row_0", "row_1", "col"))
    in_specs = (P(None, ROW, "col"), P(None, ROW, "col"))
    out_specs = (P(ROW, "col"), P(ROW, "col"))
    return jax.shard_map(
        shards, mesh=torus, in_specs=in_specs, out_specs=out_specs, check_vma=False
    )
```

profile of v0, /device:TPU:8, one launch (start us, length us, event | category | flops | bytes accessed | tf_op | source)
XLA Modules:
  0.0 465.8 jit_solution(11836406161750740182)
XLA Ops:
  7.2 2.1 copy.14
  9.4 35.8 %all-gather.4.cloned.1.call-done = bf16[4,112,3584]{1,2,0:T(8,128)(2,1)} async-done(((bf16[4,112,448]{1,2,0:T(8,128)(2,1)}), bf16[4,112,3584]{1,2,0:T(8,128)(2,1)}) %all-gather.4.cloned.1.call-update) | async-done | bytes 3211280 | tf_op jit(solution)/shard_map/all_gather | solution.py:40
  45.1 8.9 %convolution_bitcast_fusion = f32[3584,896]{1,0:T(8,128)} fusion(bf16[4,112,3584]{1,2,0:T(8,128)(2,1)} %all-gather.4.cloned.1.call-done, bf16[4,112,896]{2,1,0:T(8,128)(2,1)S(1)} %copy-done), kind=kOutput, calls=%fused_computation.2 | convolution fusion | flops 2877292544 | bytes 16859136 | tf_op jit(solution)/shard_map/mrk,mrc->kc/dot_general | solution.py:49
  54.1 118.0 %reduce-scatter.3.cloned.1.call-done = f32[896,896]{1,0:T(8,128)} async-done(((f32[3584,896]{1,0:T(8,128)}), f32[896,896]{1,0:T(8,128)}) %reduce-scatter.3.cloned.1.call-update) | async-done | bytes 3211280 | tf_op jit(solution)/shard_map/reduce_scatter | solution.py:13
  172.2 0.9 constant_dynamic-slice_fusion.1
  173.1 3.2 copy.15
  176.3 2.9 gather_fusion
  179.2 0.6 fusion.2
  179.8 43.2 %reduce-scatter.5.cloned.1.call-done = f32[112,896]{1,0:T(8,128)} async-done(((f32[896,896]{1,0:T(8,128)}), f32[112,896]{1,0:T(8,128)}) %reduce-scatter.5.cloned.1.call-update) | async-done | bytes 401424 | tf_op jit(solution)/shard_map/reduce_scatter | solution.py:13
  223.1 1.8 fusion.10
  224.9 3.0 convert_reduce_fusion
  228.1 1.7 gather_fusion.1
  229.8 83.2 %all-gather.6.cloned.1.call-done = bf16[3584,896]{1,0:T(8,128)(2,1)} async-done(((bf16[112,896]{1,0:T(8,128)(2,1)}), bf16[3584,896]{1,0:T(8,128)(2,1)}) %all-gather.6.cloned.1.call-update) | async-done | bytes 6422544 | tf_op jit(solution)/shard_map/all_gather | solution.py:58
  313.0 6.9 %multiply_reduce_fusion.6 = (f32[896]{0:T(1024)S(1)}, f32[896]{0:T(1024)S(1)}, f32[896]{0:T(1024)S(1)}, f32[112,896]{1,0:T(8,128)}) fusion(f32[112,896]{1,0:T(8,128)S(1)} %get-tuple-element.14, bf16[112,896]{1,0:T(8,128)(2,1)S(1)} %copy-done.1, f32[112]{0:T(128)S(1)} %broadcast_multiply_fusion, f32[112,3584]{0,1:T(8,128)S(1)} %convert_reduce_fusion, ...), kind=kOutput, calls=%fused_computation.22 | convolution fusion | flops 4316939776 | bytes 9042880 | tf_op jit(solution)/shard_map/dot_general | solution.py:60
  319.9 0.2 broadcast_in_dim.12
  320.2 21.0 %all_to_all.12 = f32[32,1,3584]{2,1,0:T(1,128)S(1)} all-to-all(f32[32,1,3584]{2,1,0:T(1,128)S(1)} %broadcast_in_dim.12), channel_id=1, replica_groups=mesh['row_0'=4,'row_1'=8,'col'=8] {'row_0','row_1'}, dimensions={0} | all-to-all | bytes 917504 | tf_op jit(solution)/shard_map/all_to_all | solution.py:19
  341.2 0.3 reduce_sum.98
  341.5 1.7 fusion.5
  343.3 85.4 %all-gather.8.cloned.1.call-done = bf16[3584,896]{1,0:T(8,128)(2,1)} async-done(((bf16[112,896]{1,0:T(8,128)(2,1)}), bf16[3584,896]{1,0:T(8,128)(2,1)}) %all-gather.8.cloned.1.call-update) | async-done | bytes 6422544 | tf_op jit(solution)/shard_map/all_gather | solution.py:58
  428.7 7.0 %multiply_reduce_fusion.3 = (f32[896]{0:T(1024)S(1)}, f32[896]{0:T(1024)S(1)}, f32[896]{0:T(1024)S(1)}, f32[896]{0:T(1024)S(1)}, f32[112,896]{1,0:T(8,128)}) fusion(f32[112,896]{1,0:T(8,128)S(1)} %get-tuple-element.10, f32[112,896]{1,0:T(8,128)S(1)} %get-tuple-element.14, f32[896]{0:T(1024)S(1)} %get-tuple-element.11, ...), kind=kOutput, calls=%fused_computation.17 | convolution fusion | flops 4317340160 | bytes 9451456 | tf_op jit(solution)/shard_map/dot_general | solution.py:60
  435.7 0.2 broadcast_in_dim.13
  436.0 21.0 %all_to_all.13 = f32[32,1,3584]{2,1,0:T(1,128)S(1)} all-to-all(f32[32,1,3584]{2,1,0:T(1,128)S(1)} %broadcast_in_dim.13), channel_id=1, replica_groups=mesh['row_0'=4,'row_1'=8,'col'=8] {'row_0','row_1'}, dimensions={0} | all-to-all | bytes 917504 | tf_op jit(solution)/shard_map/all_to_all | solution.py:19
  457.0 0.3 reduce_sum.103
  457.3 2.0 multiply_subtract_fusion
  (22 shorter events, 0.4 us)
Async XLA Ops:
  7.2 38.0 %copy-start = (bf16[4,112,896]{2,1,0:T(8,128)(2,1)S(1)}, bf16[4,112,896]{2,1,0:T(8,128)(2,1)}, u32[]{:S(2)}) copy-start(bf16[4,112,896]{2,1,0:T(8,128)(2,1)} %param.3) | copy-start | bytes 2408452
  7.2 38.0 %all-gather.4.cloned.1.call-start = ((), (), s32[]{:S(2)}) async-start(), calls=%async_computation.4 | async-start | bytes 4128768 | tf_op jit(solution)/shard_map/all_gather | solution.py:40
  9.3 162.8 %reduce-scatter.3.cloned.1.call-start = ((), (), s32[]{:S(2)}) async-start(), calls=%async_computation.5 | async-start | bytes 16056320 | tf_op jit(solution)/shard_map/reduce_scatter | solution.py:13
  54.0 169.0 %reduce-scatter.5.cloned.1.call-start = ((), (), s32[]{:S(2)}) async-start(), calls=%async_computation.6 | async-start | bytes 3612672 | tf_op jit(solution)/shard_map/reduce_scatter | solution.py:13
  172.1 140.9 %all-gather.6.cloned.1.call-start = ((), (), s32[]{:S(2)}) async-start(), calls=%async_computation.7 | async-start | bytes 6623232 | tf_op jit(solution)/shard_map/all_gather | solution.py:58
  224.8 88.2 %copy-start.1 = (bf16[112,896]{1,0:T(8,128)(2,1)S(1)}, bf16[112,896]{1,0:T(8,128)(2,1)}, u32[]{:S(2)}) copy-start(bf16[112,896]{1,0:T(8,128)(2,1)} %get-tuple-element.13) | copy-start | bytes 602116
  224.9 203.8 %all-gather.8.cloned.1.call-start = ((), (), s32[]{:S(2)}) async-start(), calls=%async_computation.8 | async-start | bytes 6623232 | tf_op jit(solution)/shard_map/all_gather | solution.py:58
Sparse Core Ops, SparseCore 0:
  9.8 35.2 all-gather.3
  54.2 117.8 reduce-scatter.2
  174.6 48.3 reduce-scatter.4
  226.1 86.8 all-gather.5
  343.4 85.2 all-gather.7
where the time goes:
time: 468 us; the launch traced here: 466 us
  waiting for transfers between devices  366 us (78%)
  blocking collectives  42 us (9%)
  matrix products  23.4 us (5%)
  between operations  13.9 us (3%)
  local copies, waits for them, and re-layouts  11.4 us (2%)
  other arithmetic  9.11 us (2%)
    all_gather x2, waiting for transfers between devices, shards(): shard_piece = lax.all_gather(rounded, ROW, axis=0, tiled=True)  169 us
    reduce_scatter x2, waiting for transfers between devices, sum_by_axis(): so_far = lax.psum_scatter(so_far, axis, scatter_dimension=0, tiled=True)  161 us
    all_to_all x2, blocking collectives, sent_to_all(): return lax.all_to_all(copies, axis, split_axis=0, concat_axis=0, tiled=True)  42 us
    all_gather x1, waiting for transfers between devices, shards(): gram_slabs = lax.all_gather(grams, 'col', axis=2, tiled=True)  35.8 us
    dot_general x2, matrix products, shards(): jnp.dot(add_columns, shard_piece.astype(jnp.float32), precision=high)  14 us
  transfers between devices with their start and end apart: 5, of which 5 were waited for; matrix products, arithmetic and copies ran while one was open for 3% of the time, Pallas kernels for 0%

commit v1 on v0

v1 whole, which is shorter than its diff:
```python
import functools

import jax
import jax.numpy as jnp
from jax import lax
from jax.experimental import pallas as pl
from jax.experimental.pallas import tpu as pltpu
from jax.sharding import Mesh
from jax.sharding import PartitionSpec as P

MESH = pl.DeviceIdType.MESH
F32 = jnp.float32
BF16 = jnp.bfloat16

NX, NY, NZ = 4, 4, 8
M = 4
R = 112
LANES = 128
HALF = 4 * R
CHUNKS = 7
F_LO, F_HI = pl.ds(0, 56), pl.ds(56, 56)
B_LO, B_HI = pl.ds(0, 64), pl.ds(64, 48)

RSZ = 0
AGZ = 8
RSY = 24
STY = 32
STZ = 38
KINDS = 52


def kernel(
    g_ref,
    w_ref,
    merged_ref,
    resid_ref,
    gt,
    t_hi,
    t_lo,
    diag,
    wb,
    cb,
    rz,
    d1,
    d2,
    pb,
    ry,
    res,
    dirn,
    mapped,
    merged,
    sty,
    stz,
    q_send,
    q_recv,
    e_send,
    e_recv,
    w_send,
    w_recv,
    s_send,
    s_recv,
):
    x, y, z, c = (lax.axis_index(a) for a in ("x", "y", "z", "c"))
    other = 1 - c
    z_half, z_quarter = lax.div(z, 4), lax.rem(z, 4)
    home = z_half == c

    def at(axis, index, step, size):
        return {axis: lax.rem(index + (step + size), size)}

    xp, xm = at("x", x, 1, NX), at("x", x, -1, NX)
    yp, ym = at("y", y, 1, NY), at("y", y, -1, NY)
    zp, zm = at("z", z, 1, NZ), at("z", z, -1, NZ)

    def zi(step):
        return lax.rem(z + (step + NZ), NZ)

    def yi(step):
        return lax.rem(y + (step + NY), NY)

    def xi(step):
        return lax.rem(x + (step + NX), NX)

    def copy(src, dst, send, recv, device):
        return pltpu.make_async_remote_copy(
            src_ref=src, dst_ref=dst, send_sem=send, recv_sem=recv, device_id=device, device_id_type=MESH
        )

    barrier = pltpu.get_barrier_semaphore()
    for dz in range(NZ):
        for dc in range(2):
            if dz or dc:
                pl.semaphore_signal(
                    barrier, inc=1, device_id={"z": zi(dz), "c": lax.rem(c + dc, 2)}, device_id_type=MESH
                )
    for d in (1, 2, 3):
        pl.semaphore_signal(barrier, inc=1, device_id=at("y", y, d, NY), device_id_type=MESH)
    for device in (xp, xm):
        pl.semaphore_signal(barrier, inc=1, device_id=device, device_id_type=MESH)
    pl.semaphore_wait(barrier, 2 * NZ - 1 + 3 + 2)

    def w_copy(j, way):
        lanes = pl.ds(j * LANES, LANES)
        return copy(
            w_ref.at[:, :, lanes], wb.at[j, y, :, pl.ds(0, R), :], w_send.at[way, j], w_recv.at[way, j], (yp, ym)[way]
        )

    def w_arrival(j, way):
        dst = wb.at[j, yi(-1 if way == 0 else 1), :, pl.ds(0, R), :]
        return copy(dst, dst, w_send.at[way, j], w_recv.at[way, j], (yp, ym)[way])

    def w_forward(j, way):
        models = pl.ds(0, 2) if way == 0 else pl.ds(2, 2)
        dst = wb.at[j, yi(-1 if way == 0 else 1), models, pl.ds(0, R), :]
        return copy(dst, dst, w_send.at[2 + way, j], w_recv.at[2 + way, j], (yp, ym)[way])

    def w_far(j, way):
        models = pl.ds(0, 2) if way == 0 else pl.ds(2, 2)
        dst = wb.at[j, yi(2), models, pl.ds(0, R), :]
        return copy(dst, dst, w_send.at[2 + way, j], w_recv.at[2 + way, j], (yp, ym)[way])

    def q_copy(m, quarter):
        return copy(
            g_ref.at[quarter, m],
            gt.at[z_half, x, m, pl.ds(pl.multiple_of(z_quarter * R, 16), R), :],
            q_send.at[m, quarter],
            q_recv.at[m, z_quarter],
            {"z": 4 * c + quarter, "c": z_half},
        )

    def q_arrival(m, quarter):
        dst = gt.at[c, x, m, pl.ds(quarter * R, R), :]
        return copy(dst, dst, q_send.at[m, quarter], q_recv.at[m, quarter], {"z": 4 * c + quarter, "c": z_half})

    def away(quarter):
        return jnp.logical_not(jnp.logical_and(home, z_quarter == quarter))

    for m in range(M):
        for quarter in range(4):

            @pl.when(away(quarter))
            def _():
                q_copy(m, quarter).start()

    for j in range(CHUNKS):
        for way in range(2):
            w_copy(j, way).start()

    @pl.when(home)
    def _():
        rows = pl.ds(pl.multiple_of(z_quarter * R, 16), R)
        for m in range(M):
            gt[z_half, x, m, rows, :] = g_ref[z_quarter, m]

    for j in range(CHUNKS):
        for m in range(M):
            wb[j, y, m, pl.ds(0, R), :] = w_ref[m, :, j * LANES : (j + 1) * LANES]
            for k in range(NY):
                wb[j, k, m, pl.ds(R, LANES - R), :] = jnp.zeros((LANES - R, LANES), BF16)

    def e_copy(m, offset, kind, device):
        ref = gt.at[c, xi(offset), m]
        return copy(ref, ref, e_send.at[kind, m], e_recv.at[kind, m], device)

    def e_from_core(m, k):
        ref = gt.at[other, xi(k), m]
        return copy(ref, ref, e_send.at[3 + k, m], e_recv.at[3 + k, m], {"c": other})

    def to_core(m, k):
        return e_copy(m, k, 3 + k, {"c": other})

    for m in range(M):
        for quarter in range(4):

            @pl.when(away(quarter))
            def _():
                q_arrival(m, quarter).wait_recv()

        e_copy(m, 0, 0, xp).start()
        e_copy(m, 0, 1, xm).start()
        to_core(m, 0).start()
    for j in range(2):
        for way in range(2):
            w_arrival(j, way).wait_recv()
            w_forward(j, way).start()
    for m in (0, 2, 1, 3):
        e_copy(m, -1, 0, xp).wait_recv()
        if m < 2:
            e_copy(m, -1, 2, xp).start()
        to_core(m, 3).start()
        e_copy(m, 1, 1, xm).wait_recv()
        if m >= 2:
            e_copy(m, 1, 2, xm).start()
        to_core(m, 1).start()
    for j in range(2, CHUNKS):
        for way in range(2):
            w_arrival(j, way).wait_recv()
            w_forward(j, way).start()
    for m in (0, 2, 1, 3):
        e_copy(m, 2, 2, xp).wait_recv()
        to_core(m, 2).start()
    for m in range(M):
        for k in range(NX):
            e_from_core(m, k).wait_recv()

    for k in range(NX):
        total = jnp.concatenate(
            [
                gt[h, k, 0].astype(F32) + gt[h, k, 1].astype(F32) + gt[h, k, 2].astype(F32) + gt[h, k, 3].astype(F32)
                for h in range(2)
            ],
            axis=0,
        )
        total = jnp.transpose(total)[:R]
        high = total.astype(BF16)
        t_hi[k * R : (k + 1) * R, :] = high
        t_lo[k * R : (k + 1) * R, :] = (total - high.astype(F32)).astype(BF16)
    on_diag = lax.broadcasted_iota(jnp.int32, (R, LANES), 0) == lax.broadcasted_iota(jnp.int32, (R, LANES), 1)
    diag_total = jnp.zeros((R, LANES), F32)
    for m in range(M):
        block = gt[z_half, y, m, pl.ds(pl.multiple_of(z_quarter * R, 16), R), :].astype(F32)
        values = jnp.sum(jnp.where(on_diag, block, 0.0), axis=1, keepdims=True)
        values = jnp.broadcast_to(values, (R, LANES))
        diag[m] = values
        diag_total = diag_total + values
    diag[M] = diag_total

    def message(kind, j, src, dst, device):
        return copy(src, dst, s_send.at[kind], s_recv.at[kind, j], device)

    def arrived(kind, j, dst, device):
        copy(dst, dst, s_send.at[kind], s_recv.at[kind, j], device).wait_recv()

    def sent(kind, j, src, device):
        copy(src, src, s_send.at[kind], s_recv.at[kind, j], device).wait_send()

    def rsz(j, step, way):
        sign = 1 if way == 0 else -1
        t = zi(sign * (5 - step))
        rows = pl.ds(0, R) if step > 1 else (F_LO, F_HI)[way]
        kind = RSZ + 2 * (step - 1) + way
        return kind, cb.at[j, t, rows, :], rz.at[way, j, step - 1, rows, :], (zp, zm)[way]

    def rsz_start(j, step):
        for way in range(2):
            kind, src, dst, device = rsz(j, step, way)
            message(kind, j, src, dst, device).start()

    def rsz_wait(j, step):
        for way in range(2):
            kind, src, dst, device = rsz(j, step, way)
            arrived(kind, j, dst, device)
            sent(kind, j, src, device)

    def right_partial(j):
        for way in range(2):
            w_far(j, way).wait_recv()
        for h in range(2):
            acc = jnp.zeros((HALF, LANES), F32)
            for k in range(NY):
                for m in (0, 2):
                    lhs = jnp.concatenate([gt[h, k, m], gt[h, k, m + 1]], axis=1)
                    rhs = jnp.concatenate([wb[j, k, m], wb[j, k, m + 1]], axis=0)
                    acc = acc + jnp.dot(lhs, rhs, preferred_element_type=F32)
            for q in range(4):
                cb[j, 4 * h + q] = acc[q * R : (q + 1) * R]
        rsz_start(j, 1)

    def right_step(step, j):
        rsz_wait(j, step - 1)
        plus, minus = zi(5 - step), zi(step - 5)
        if step == 2:
            cb[j, plus, F_LO, :] += rz[0, j, 0, F_LO, :]
            cb[j, minus, F_HI, :] += rz[1, j, 0, F_HI, :]
        else:
            cb[j, plus] += rz[0, j, step - 2]
            cb[j, minus] += rz[1, j, step - 2]
        rsz_start(j, step)

    def own_rows(index):
        return pl.multiple_of(index * R, 16)

    def agz(it, j, step, way, arriving):
        sign = -1 if way == 0 else 1
        origin = zi(sign * (step if arriving else step - 1))
        first, count = (0, R) if step < 4 else ((0, 64), (64, 48))[way]
        kind = AGZ + 8 * it + 2 * (step - 1) + way
        ref = (d1, d2)[it].at[j, pl.ds(pl.multiple_of(origin * R + first, 16), count), :]
        return kind, ref, (zp, zm)[way]

    def agz_start(it, j, step):
        for way in range(2):
            kind, ref, device = agz(it, j, step, way, False)
            message(kind, j, ref, ref, device).start()

    def agz_wait(it, j, step):
        for way in range(2):
            kind, ref, device = agz(it, j, step, way, True)
            arrived(kind, j, ref, device)
            kind, ref, device = agz(it, j, step, way, False)
            sent(kind, j, ref, device)

    def right_end(j):
        rsz_wait(j, 4)
        product = cb[j, z] + rz[0, j, 3] + rz[1, j, 3]
        on_diag_sum = jnp.zeros((R, LANES), F32)
        for m in range(M):
            on_diag_sum = on_diag_sum + diag[m] * wb[j, y, m, pl.ds(0, R), :].astype(F32)
        right = 0.9 * product + 0.1 * on_diag_sum
        res[j] = right
        dirn[j] = right
        d1[j, pl.ds(own_rows(z), R), :] = right.astype(BF16)
        agz_start(0, j, 1)

    def pass_on(it, step, j):
        agz_wait(it, j, step - 1)
        agz_start(it, j, step)

    def rsy(it, j, step, way):
        t = yi(2 if step == 1 else (1 if way == 0 else -1))
        rows = pl.ds(0, R) if step > 1 else (F_LO, F_HI)[way]
        kind = RSY + 4 * it + 2 * (step - 1) + way
        return kind, pb.at[it, j, t, rows, :], ry.at[it, way, j, step - 1, rows, :], (yp, ym)[way]

    def rsy_start(it, j, step):
        for way in range(2):
            kind, src, dst, device = rsy(it, j, step, way)
            message(kind, j, src, dst, device).start()

    def rsy_wait(it, j, step):
        for way in range(2):
            kind, src, dst, device = rsy(it, j, step, way)
            arrived(kind, j, dst, device)
            sent(kind, j, src, device)

    def map_partial(it, j):
        agz_wait(it, j, 4)
        d = (d1, d2)[it][j]
        out = jnp.dot(t_hi[...], d, preferred_element_type=F32) + jnp.dot(t_lo[...], d, preferred_element_type=F32)
        for q in range(NY):
            pb[it, j, q] = out[q * R : (q + 1) * R]
        rsy_start(it, j, 1)

    def map_step(it, j):
        rsy_wait(it, j, 1)
        pb[it, j, yi(1), F_LO, :] += ry[it, 0, j, 0, F_LO, :]
        pb[it, j, yi(-1), F_HI, :] += ry[it, 1, j, 0, F_HI, :]
        rsy_start(it, j, 2)

    def sty_message(it, j, d):
        return STY + 3 * it + d - 1, sty.at[it, j, y], at("y", y, d, NY)

    def stz_message(it, j, d):
        return STZ + 7 * it + d - 1, stz.at[it, j, z], at("z", z, d, NZ)

    def map_end(it, j):
        rsy_wait(it, j, 2)
        product = pb[it, j, y] + ry[it, 0, j, 1] + ry[it, 1, j, 1]
        rounded = (d1, d2)[it][j, pl.ds(own_rows(z), R), :].astype(F32)
        value = 0.9 * product + 0.1 * diag[M] * rounded
        mapped[j] = value
        r = res[j]
        norm = jnp.sum(r * r, axis=0, keepdims=True)
        curvature = jnp.sum(dirn[j] * value, axis=0, keepdims=True)
        square = jnp.sum(value * value, axis=0, keepdims=True)
        cross = jnp.sum(r * value, axis=0, keepdims=True)
        sty[it, j, y] = jnp.concatenate([norm, curvature, square, cross], axis=0)
        for d in (1, 2, 3):
            kind, ref, device = sty_message(it, j, d)
            message(kind, j, ref, ref, device).start()

    def sum_z(it, j):
        for d in (1, 2, 3):
            kind, ref, device = sty_message(it, j, d)
            arrived(kind, j, sty.at[it, j, yi(-d)], device)
            sent(kind, j, ref, device)
        stz[it, j, z] = (sty[it, j, 0] + sty[it, j, 1]) + (sty[it, j, 2] + sty[it, j, 3])
        for d in range(1, NZ):
            kind, ref, device = stz_message(it, j, d)
            message(kind, j, ref, ref, device).start()

    def update(it, j):
        for d in range(1, NZ):
            kind, ref, device = stz_message(it, j, d)
            arrived(kind, j, stz.at[it, j, zi(-d)], device)
            sent(kind, j, ref, device)
        sums = stz[it, j, 0]
        for k in range(1, NZ):
            sums = sums + stz[it, j, k]
        norm, curvature, square, cross = (sums[k : k + 1] for k in range(4))
        step = norm / curvature
        direction = dirn[j]
        residual = res[j] - step * mapped[j]
        if it == 0:
            norm_next = norm - 2.0 * step * cross + step * step * square
            merged[j] = step * direction
            direction = residual + norm_next / norm * direction
            res[j] = residual
            dirn[j] = direction
            d2[j, pl.ds(own_rows(z), R), :] = direction.astype(BF16)
            agz_start(1, j, 1)
        else:
            lanes = pl.ds(pl.multiple_of(j * LANES, LANES), LANES)
            merged_ref[:, lanes] = merged[j] + step * direction
            resid_ref[:, lanes] = residual

    stages = [right_partial]
    stages += [functools.partial(right_step, step) for step in (2, 3, 4)]
    stages += [right_end]
    for it in range(2):
        stages += [functools.partial(pass_on, it, step) for step in (2, 3, 4)]
        stages += [functools.partial(f, it) for f in (map_partial, map_step, map_end, sum_z, update)]

    def tick(t, carry):
        for s in reversed(range(len(stages))):
            j = t - s

            @pl.when(jnp.logical_and(j >= 0, j < CHUNKS))
            def _():
                stages[s](j)

        return carry

    lax.fori_loop(0, CHUNKS + len(stages) - 1, tick, 0)

    for m in range(M):
        for quarter in range(4):

            @pl.when(away(quarter))
            def _():
                q_copy(m, quarter).wait_send()

        e_copy(m, 0, 0, xp).wait_send()
        e_copy(m, 0, 1, xm).wait_send()
        if m < 2:
            e_copy(m, -1, 2, xp).wait_send()
        else:
            e_copy(m, 1, 2, xm).wait_send()
        for k in range(NX):
            to_core(m, k).wait_send()
    for j in range(CHUNKS):
        for way in range(2):
            w_copy(j, way).wait_send()
            w_forward(j, way).wait_send()


def shards(grams, weights):
    sub = grams.reshape(M, R, 4, R).transpose(2, 0, 1, 3)
    sub = jnp.pad(sub, ((0, 0), (0, 0), (0, 0), (0, LANES - R)))
    block = jax.ShapeDtypeStruct((R, CHUNKS * LANES), F32)
    vmem = pl.BlockSpec(memory_space=pltpu.VMEM)
    dma = pltpu.SemaphoreType.DMA
    return pl.pallas_call(
        kernel,
        out_shape=(block, block),
        in_specs=[vmem, vmem],
        out_specs=(vmem, vmem),
        scratch_shapes=[
            pltpu.VMEM((2, NX, M, HALF, LANES), BF16),
            pltpu.VMEM((HALF, 2 * HALF), BF16),
            pltpu.VMEM((HALF, 2 * HALF), BF16),
            pltpu.VMEM((M + 1, R, LANES), F32),
            pltpu.VMEM((CHUNKS, NY, M, LANES, LANES), BF16),
            pltpu.VMEM((CHUNKS, NZ, R, LANES), F32),
            pltpu.VMEM((2, CHUNKS, 4, R, LANES), F32),
            pltpu.VMEM((CHUNKS, 2 * HALF, LANES), BF16),
            pltpu.VMEM((CHUNKS, 2 * HALF, LANES), BF16),
            pltpu.VMEM((2, CHUNKS, NY, R, LANES), F32),
            pltpu.VMEM((2, 2, CHUNKS, 2, R, LANES), F32),
            pltpu.VMEM((CHUNKS, R, LANES), F32),
            pltpu.VMEM((CHUNKS, R, LANES), F32),
            pltpu.VMEM((CHUNKS, R, LANES), F32),
            pltpu.VMEM((CHUNKS, R, LANES), F32),
            pltpu.VMEM((2, CHUNKS, NY, 4, LANES), F32),
            pltpu.VMEM((2, CHUNKS, NZ, 4, LANES), F32),
            dma((M, 4)),
            dma((M, 4)),
            dma((7, M)),
            dma((7, M)),
            dma((4, CHUNKS)),
            dma((4, CHUNKS)),
            dma((KINDS,)),
            dma((KINDS, CHUNKS)),
        ],
        compiler_params=pltpu.CompilerParams(
            collective_id=0, has_side_effects=True, vmem_limit_bytes=56 * 1024 * 1024
        ),
    )(sub, weights)


def solution(mesh):
    torus = Mesh(mesh.devices.reshape(NY, NZ, NX, 2), ("y", "z", "x", "c"))
    spec = P(None, ("y", "z"), ("x", "c"))
    out = P(("y", "z"), ("x", "c"))
    return jax.shard_map(shards, mesh=torus, in_specs=(spec, spec), out_specs=(out, out), check_vma=False)
```

time: 468 us -> 168 us (0.36)
  waiting for transfers between devices: 366 us -> 0 us
  Pallas kernels: 0 us -> 162 us
  blocking collectives: 42 us -> 0 us
  matrix products: 23.4 us -> 0 us
  between operations: 13.9 us -> 0.65 us
  other arithmetic: 9.11 us -> 0 us
  local copies, waits for them, and re-layouts: 11.4 us -> 4.96 us
    all_gather x3 -> x0, waiting for transfers between devices: 204 us -> none  [the longest x2 169 us: shards(): shard_piece = lax.all_gather(rounded, ROW, axis=0, tiled=True)]
    pallas_call x0 -> x1, Pallas kernels: none -> 162 us  [shards(): pl.pallas_call(kernel, out_shape=(block, block), in_specs=[vmem, vmem], o...]
    reduce_scatter x2 -> x0, waiting for transfers between devices: 161 us -> none  [sum_by_axis(): so_far = lax.psum_scatter(so_far, axis, scatter_dimension=0, tiled=True)]
    all_to_all x2 -> x0, blocking collectives: 42 us -> none  [sent_to_all(): return lax.all_to_all(copies, axis, split_axis=0, concat_axis=0, tiled=True)]
    dot_general x4 -> x0, matrix products: 23.4 us -> none  [the longest x2 14 us: shards(): jnp.dot(add_columns, shard_piece.astype(jnp.float32), precision=high)]
  transfers between devices with their start and end apart: 5 -> 0, of which waited for: 5 -> 0; matrix products, arithmetic and copies ran while one was open for 3% -> 0% of each run, Pallas kernels for 0% -> 0%
where the time goes in v1:
time: 168 us
  Pallas kernels  162 us (96%)
  local copies, waits for them, and re-layouts  4.96 us (3%)
    pallas_call x1, Pallas kernels, shards(): pl.pallas_call(kernel, out_shape=(block, block), in_specs=[vmem, vmem], o...  162 us
    unnamed x5, local copies, waits for them, and re-layouts  3.85 us

profile of v1, /device:TPU:8, one launch (start us, length us, event | category | flops | bytes accessed | tf_op | source)
XLA Modules:
  0.0 167.7 jit_solution(12531163802177922730)
XLA Ops:
  0.6 1.3 copy.4
  1.9 0.2 copy.5
  2.2 0.9 pad.4.g_ref
  3.0 162.0 %shard_map.41 = (f32[112,896]{1,0:T(8,128)}, f32[112,896]{1,0:T(8,128)}) custom-call(bf16[4,4,112,128]{3,2,1,0:T(8,128)(2,1)} %pad.4.g_ref, bf16[4,112,896]{2,1,0:T(8,128)(2,1)} %w_ref.1), custom_call_target="tpu_custom_call" | custom-call | tf_op jit(solution)/shard_map/pallas_call | solution.py:453
  165.1 0.0 copy-start
  165.1 1.8 %copy.8 = f32[112,896]{1,0:T(8,128)} copy(f32[112,896]{1,0:T(8,128)} %get-tuple-element.4) | data formatting | bytes 802816
  166.9 0.0 copy-done
  166.9 0.7 copy.9
Async XLA Ops:
  165.1 1.8 %copy-start = (f32[112,896]{1,0:T(8,128)S(1)}, f32[112,896]{1,0:T(8,128)}, u32[]{:S(2)}) copy-start(f32[112,896]{1,0:T(8,128)} %get-tuple-element.5) | copy-start | bytes 1204228

commit v2 on v1

v2 whole, which is shorter than its diff:
```python
import functools

import jax
import jax.numpy as jnp
from jax import lax
from jax.experimental import pallas as pl
from jax.experimental.pallas import tpu as pltpu
from jax.sharding import Mesh
from jax.sharding import PartitionSpec as P

MESH = pl.DeviceIdType.MESH
F32 = jnp.float32
BF16 = jnp.bfloat16

NX, NY, NZ = 4, 4, 8
M = 4
R = 112
LANES = 128
HALF = 4 * R
CHUNKS = 7
F_LO, F_HI = pl.ds(0, 56), pl.ds(56, 56)

GATHER = ("ring", "hybrid")
RSY_DIRECT = True
DELAY_RIGHT = (0, 0, 0, 0, 0)
DELAY = ((0, 0, 0, 0, 0, 0, 0), (0, 0, 0, 0, 0))
STAGES = 20


def kernel(
    g_ref,
    w_ref,
    merged_ref,
    resid_ref,
    gt,
    t_hi,
    t_lo,
    diag,
    wb,
    cb,
    rz,
    d1,
    d2,
    pb,
    ry,
    res,
    dirn,
    mapped,
    merged,
    sty,
    stz,
    q_send,
    q_recv,
    e_send,
    e_recv,
    core_recv,
    w_send,
    w_recv,
    s_send,
    s_recv,
):
    x, y, z, c = (lax.axis_index(a) for a in ("x", "y", "z", "c"))
    other = 1 - c
    z_half, z_quarter = lax.div(z, 4), lax.rem(z, 4)
    home = z_half == c

    def at(axis, index, step, size):
        return {axis: lax.rem(index + (step + size), size)}

    xp, xm = at("x", x, 1, NX), at("x", x, -1, NX)
    yp, ym = at("y", y, 1, NY), at("y", y, -1, NY)
    zp, zm = at("z", z, 1, NZ), at("z", z, -1, NZ)

    def zi(step):
        return lax.rem(z + (step + NZ), NZ)

    def yi(step):
        return lax.rem(y + (step + NY), NY)

    def xi(step):
        return lax.rem(x + (step + NX), NX)

    def copy(src, dst, send, recv, device):
        return pltpu.make_async_remote_copy(
            src_ref=src, dst_ref=dst, send_sem=send, recv_sem=recv, device_id=device, device_id_type=MESH
        )

    barrier = pltpu.get_barrier_semaphore()
    for dz in range(NZ):
        for dc in range(2):
            if dz or dc:
                pl.semaphore_signal(
                    barrier, inc=1, device_id={"z": zi(dz), "c": lax.rem(c + dc, 2)}, device_id_type=MESH
                )
    for d in (1, 2, 3):
        pl.semaphore_signal(barrier, inc=1, device_id=at("y", y, d, NY), device_id_type=MESH)
    for device in (xp, xm):
        pl.semaphore_signal(barrier, inc=1, device_id=device, device_id_type=MESH)
    pl.semaphore_wait(barrier, 2 * NZ - 1 + 3 + 2)

    def w_copy(j, way):
        lanes = pl.ds(j * LANES, LANES)
        return copy(
            w_ref.at[:, :, lanes], wb.at[j, y, :, pl.ds(0, R), :], w_send.at[way], w_recv.at[way, j], (yp, ym)[way]
        )

    def w_arrival(j, way):
        dst = wb.at[j, yi(-1 if way == 0 else 1), :, pl.ds(0, R), :]
        return copy(dst, dst, w_send.at[way], w_recv.at[way, j], (yp, ym)[way])

    def w_forward(j, way):
        models = pl.ds(0, 2) if way == 0 else pl.ds(2, 2)
        dst = wb.at[j, yi(-1 if way == 0 else 1), models, pl.ds(0, R), :]
        return copy(dst, dst, w_send.at[2 + way], w_recv.at[2 + way, j], (yp, ym)[way])

    def w_far(j, way):
        models = pl.ds(0, 2) if way == 0 else pl.ds(2, 2)
        dst = wb.at[j, yi(2), models, pl.ds(0, R), :]
        return copy(dst, dst, w_send.at[2 + way], w_recv.at[2 + way, j], (yp, ym)[way])

    def q_copy(m, quarter):
        return copy(
            g_ref.at[quarter, m],
            gt.at[z_half, x, m, pl.ds(pl.multiple_of(z_quarter * R, 16), R), :],
            q_send.at[0],
            q_recv.at[m],
            {"z": 4 * c + quarter, "c": z_half},
        )

    def q_take(m):
        for blocks, there in ((3, home), (4, jnp.logical_not(home))):

            @pl.when(there)
            def _():
                dst = gt.at[c, x, m, pl.ds(0, blocks * R), :]
                copy(dst, dst, q_send.at[0], q_recv.at[m], zp).wait_recv()

    def away(quarter):
        return jnp.logical_not(jnp.logical_and(home, z_quarter == quarter))

    for m in range(M):
        for quarter in range(4):

            @pl.when(away(quarter))
            def _():
                q_copy(m, quarter).start()

    for j in range(CHUNKS):
        for way in range(2):
            w_copy(j, way).start()

    @pl.when(home)
    def _():
        rows = pl.ds(pl.multiple_of(z_quarter * R, 16), R)
        for m in range(M):
            gt[z_half, x, m, rows, :] = g_ref[z_quarter, m]

    for j in range(CHUNKS):
        for m in range(M):
            wb[j, y, m, pl.ds(0, R), :] = w_ref[m, :, j * LANES : (j + 1) * LANES]
            for k in range(NY):
                wb[j, k, m, pl.ds(R, LANES - R), :] = jnp.zeros((LANES - R, LANES), BF16)

    def e_copy(m, offset, kind, device):
        ref = gt.at[c, xi(offset), m]
        return copy(ref, ref, e_send.at[0], e_recv.at[kind, m], device)

    def to_core(m, k):
        ref = gt.at[c, xi(k), m]
        return copy(ref, ref, e_send.at[1], core_recv.at[0], {"c": other})

    for m in range(M):
        q_take(m)
        e_copy(m, 0, 0, xp).start()
        e_copy(m, 0, 1, xm).start()
        to_core(m, 0).start()
    for j in range(2):
        for way in range(2):
            w_arrival(j, way).wait_recv()
            w_forward(j, way).start()
    for m in (0, 2, 1, 3):
        e_copy(m, -1, 0, xp).wait_recv()
        if m < 2:
            e_copy(m, -1, 2, xp).start()
        to_core(m, 3).start()
        e_copy(m, 1, 1, xm).wait_recv()
        if m >= 2:
            e_copy(m, 1, 2, xm).start()
        to_core(m, 1).start()
    for j in range(2, CHUNKS):
        for way in range(2):
            w_arrival(j, way).wait_recv()
            w_forward(j, way).start()
    for m in (0, 2, 1, 3):
        e_copy(m, 2, 2, xp).wait_recv()
        to_core(m, 2).start()
    from_core = gt.at[other]
    copy(from_core, from_core, e_send.at[1], core_recv.at[0], {"c": other}).wait_recv()

    for k in range(NX):
        total = jnp.concatenate(
            [
                gt[h, k, 0].astype(F32) + gt[h, k, 1].astype(F32) + gt[h, k, 2].astype(F32) + gt[h, k, 3].astype(F32)
                for h in range(2)
            ],
            axis=0,
        )
        total = jnp.transpose(total)[:R]
        high = total.astype(BF16)
        t_hi[k * R : (k + 1) * R, :] = high
        t_lo[k * R : (k + 1) * R, :] = (total - high.astype(F32)).astype(BF16)
    on_diag = lax.broadcasted_iota(jnp.int32, (R, LANES), 0) == lax.broadcasted_iota(jnp.int32, (R, LANES), 1)
    diag_total = jnp.zeros((R, LANES), F32)
    for m in range(M):
        block = gt[z_half, y, m, pl.ds(pl.multiple_of(z_quarter * R, 16), R), :].astype(F32)
        values = jnp.sum(jnp.where(on_diag, block, 0.0), axis=1, keepdims=True)
        values = jnp.broadcast_to(values, (R, LANES))
        diag[m] = values
        diag_total = diag_total + values
    diag[M] = diag_total

    def slot(stage, j):
        return 4 * stage + lax.rem(j, 4)

    def send(stage, j, messages):
        for ref, dst, device in messages:
            copy(ref, dst, s_send.at[slot(stage, j)], s_recv.at[slot(stage, j)], device).start()

    def take(stage, j, whole):
        both = copy(whole, whole, s_send.at[slot(stage, j)], s_recv.at[slot(stage, j)], zp)
        both.wait_recv()
        both.wait_send()

    def own_rows(index):
        return pl.multiple_of(index * R, 16)

    def rsz_send(stage, step, j):
        messages = []
        for way in range(2):
            t = zi((5 - step) if way == 0 else (step - 5))
            rows = pl.ds(0, R) if step > 1 else (F_LO, F_HI)[way]
            messages.append((cb.at[j, t, rows, :], rz.at[way, j, step - 1, rows, :], (zp, zm)[way]))
        send(stage, j, messages)

    def right_partial(stage, j):
        for way in range(2):
            w_far(j, way).wait_recv()
        for h in range(2):
            acc = jnp.zeros((HALF, LANES), F32)
            for k in range(NY):
                for m in (0, 2):
                    lhs = jnp.concatenate([gt[h, k, m], gt[h, k, m + 1]], axis=1)
                    rhs = jnp.concatenate([wb[j, k, m], wb[j, k, m + 1]], axis=0)
                    acc = acc + jnp.dot(lhs, rhs, preferred_element_type=F32)
            for q in range(4):
                cb[j, 4 * h + q] = acc[q * R : (q + 1) * R]
        rsz_send(stage, 1, j)

    def right_step(step, stage, j):
        take(stage - 1, j, cb.at[j, 0] if step == 2 else cb.at[j, pl.ds(0, 2)])
        plus, minus = zi(5 - step), zi(step - 5)
        if step == 2:
            cb[j, plus, F_LO, :] += rz[0, j, 0, F_LO, :]
            cb[j, minus, F_HI, :] += rz[1, j, 0, F_HI, :]
        else:
            cb[j, plus] += rz[0, j, step - 2]
            cb[j, minus] += rz[1, j, step - 2]
        rsz_send(stage, step, j)

    def d_rows(it, j, step, first=0, count=R):
        return (d1, d2)[it].at[j, pl.ds(pl.multiple_of(zi(step) * R + first, 16), count), :]

    def same(ref, device):
        return ref, ref, device

    LO, HI = (0, 64), (64, 48)
    zpp, zmm = at("z", z, 2, NZ), at("z", z, -2, NZ)

    def gather_start(it, stage, j):
        own = d_rows(it, j, 0)
        devices = [zp, zm]
        if GATHER[it] == "hybrid":
            devices += [zpp, zmm]
        elif GATHER[it] == "direct":
            devices = [at("z", z, d, NZ) for d in (4, 3, -3, 2, -2, 1, -1)]
        send(stage, j, [same(own, device) for device in devices])

    def gather_steps(it):
        ref = (d1, d2)[it]

        def ring(step, stage, j):
            take(stage - 1, j, ref.at[j, pl.ds(0, 2 * R), :])
            near, far = (1 - step, step - 1)
            parts = (LO, HI) if step == 4 else ((0, R), (0, R))
            send(stage, j, [same(d_rows(it, j, near, *parts[0]), zp), same(d_rows(it, j, far, *parts[1]), zm)])

        def hybrid(stage, j):
            take(stage - 1, j, ref.at[j, pl.ds(0, 4 * R), :])
            send(
                stage,
                j,
                [
                    same(d_rows(it, j, -2), zp),
                    same(d_rows(it, j, 2), zm),
                    same(d_rows(it, j, -2, *LO), zpp),
                    same(d_rows(it, j, 2, *HI), zmm),
                ],
            )

        if GATHER[it] == "ring":
            return [functools.partial(ring, step) for step in (2, 3, 4)], R
        if GATHER[it] == "hybrid":
            return [hybrid], 3 * R
        return [], 7 * R

    def right_end(stage, j):
        take(stage - 1, j, cb.at[j, pl.ds(0, 2)])
        product = cb[j, z] + rz[0, j, 3] + rz[1, j, 3]
        on_diag_sum = jnp.zeros((R, LANES), F32)
        for m in range(M):
            on_diag_sum = on_diag_sum + diag[m] * wb[j, y, m, pl.ds(0, R), :].astype(F32)
        right = 0.9 * product + 0.1 * on_diag_sum
        res[j] = right
        dirn[j] = right
        d1[j, pl.ds(own_rows(z), R), :] = right.astype(BF16)
        gather_start(0, stage, j)

    def map_partial(it, last_rows, stage, j):
        ref = (d1, d2)[it]
        take(stage - 1, j, ref.at[j, pl.ds(0, last_rows), :])
        d = ref[j]
        out = jnp.dot(t_hi[...], d, preferred_element_type=F32) + jnp.dot(t_lo[...], d, preferred_element_type=F32)
        for q in range(NY):
            pb[it, j, q] = out[q * R : (q + 1) * R]
        if RSY_DIRECT:
            send(
                stage,
                j,
                [(pb.at[it, j, yi(d)], ry.at[it, j, d - 1], at("y", y, d, NY)) for d in (2, 1, 3)],
            )
        else:
            t = yi(2)
            send(
                stage,
                j,
                [
                    (pb.at[it, j, t, F_LO, :], ry.at[it, j, 1, F_LO, :], yp),
                    (pb.at[it, j, t, F_HI, :], ry.at[it, j, 1, F_HI, :], ym),
                ],
            )

    def map_step(it, stage, j):
        take(stage - 1, j, pb.at[it, j, 0])
        pb[it, j, yi(1), F_LO, :] += ry[it, j, 1, F_LO, :]
        pb[it, j, yi(-1), F_HI, :] += ry[it, j, 1, F_HI, :]
        send(
            stage,
            j,
            [(pb.at[it, j, yi(1)], ry.at[it, j, 0], yp), (pb.at[it, j, yi(-1)], ry.at[it, j, 2], ym)],
        )

    def map_end(it, stage, j):
        take(stage - 1, j, pb.at[it, j, pl.ds(0, 3 if RSY_DIRECT else 2)])
        product = pb[it, j, y] + ry[it, j, 0] + ry[it, j, 2]
        if RSY_DIRECT:
            product = product + ry[it, j, 1]
        rounded = (d1, d2)[it][j, pl.ds(own_rows(z), R), :].astype(F32)
        value = 0.9 * product + 0.1 * diag[M] * rounded
        mapped[j] = value
        r = res[j]
        norm = jnp.sum(r * r, axis=0, keepdims=True)
        curvature = jnp.sum(dirn[j] * value, axis=0, keepdims=True)
        square = jnp.sum(value * value, axis=0, keepdims=True)
        cross = jnp.sum(r * value, axis=0, keepdims=True)
        sty[it, j, y] = jnp.concatenate([norm, curvature, square, cross], axis=0)
        send(stage, j, [same(sty.at[it, j, y], at("y", y, d, NY)) for d in (2, 1, 3)])

    def sum_z(it, stage, j):
        take(stage - 1, j, sty.at[it, j, pl.ds(0, NY - 1)])
        stz[it, j, z] = (sty[it, j, 0] + sty[it, j, 1]) + (sty[it, j, 2] + sty[it, j, 3])
        send(stage, j, [same(stz.at[it, j, z], at("z", z, d, NZ)) for d in (4, 3, 5, 2, 6, 1, 7)])

    def update(it, stage, j):
        take(stage - 1, j, stz.at[it, j, pl.ds(0, NZ - 1)])
        sums = stz[it, j, 0]
        for k in range(1, NZ):
            sums = sums + stz[it, j, k]
        norm, curvature, square, cross = (sums[k : k + 1] for k in range(4))
        step = norm / curvature
        direction = dirn[j]
        residual = res[j] - step * mapped[j]
        if it == 0:
            norm_next = norm - 2.0 * step * cross + step * step * square
            merged[j] = step * direction
            direction = residual + norm_next / norm * direction
            res[j] = residual
            dirn[j] = direction
            d2[j, pl.ds(own_rows(z), R), :] = direction.astype(BF16)
            gather_start(1, stage, j)
        else:
            lanes = pl.ds(pl.multiple_of(j * LANES, LANES), LANES)
            merged_ref[:, lanes] = merged[j] + step * direction
            resid_ref[:, lanes] = residual

    stages = [right_partial]
    stages += [functools.partial(right_step, step) for step in (2, 3, 4)]
    stages += [right_end]
    delays = list(DELAY_RIGHT)
    for it in range(2):
        steps, last_rows = gather_steps(it)
        stages += steps
        stages += [functools.partial(map_partial, it, last_rows)]
        if not RSY_DIRECT:
            stages += [functools.partial(map_step, it)]
        stages += [functools.partial(f, it) for f in (map_end, sum_z, update)]
        delays += list(DELAY[it])
    assert len(stages) == len(delays) + 0
    ticks = [s + sum(delays[:s]) for s in range(len(stages))]

    def tick(t, carry):
        for s in range(len(stages)):
            j = t - ticks[s]

            @pl.when(jnp.logical_and(j >= 0, j < CHUNKS))
            def _():
                stages[s](s, j)

        return carry

    lax.fori_loop(0, CHUNKS + ticks[-1], tick, 0)

    for blocks, there in ((3, home), (4, jnp.logical_not(home))):

        @pl.when(there)
        def _():
            ref = g_ref.at[pl.ds(0, blocks)]
            copy(ref, ref, q_send.at[0], q_recv.at[0], zp).wait_send()

    along_x = gt.at[0, pl.ds(0, 3)]
    copy(along_x, along_x, e_send.at[0], e_recv.at[0, 0], xp).wait_send()
    copy(from_core, from_core, e_send.at[1], core_recv.at[0], {"c": other}).wait_send()
    for way in range(2):
        copy(w_ref, w_ref, w_send.at[way], w_recv.at[way, 0], yp).wait_send()
        ref = w_ref.at[pl.ds(0, 2)]
        copy(ref, ref, w_send.at[2 + way], w_recv.at[2 + way, 0], yp).wait_send()


def shards(grams, weights):
    sub = grams.reshape(M, R, 4, R).transpose(2, 0, 1, 3)
    sub = jnp.pad(sub, ((0, 0), (0, 0), (0, 0), (0, LANES - R)))
    block = jax.ShapeDtypeStruct((R, CHUNKS * LANES), F32)
    vmem = pl.BlockSpec(memory_space=pltpu.VMEM)
    dma = pltpu.SemaphoreType.DMA
    return pl.pallas_call(
        kernel,
        out_shape=(block, block),
        in_specs=[vmem, vmem],
        out_specs=(vmem, vmem),
        scratch_shapes=[
            pltpu.VMEM((2, NX, M, HALF, LANES), BF16),
            pltpu.VMEM((HALF, 2 * HALF), BF16),
            pltpu.VMEM((HALF, 2 * HALF), BF16),
            pltpu.VMEM((M + 1, R, LANES), F32),
            pltpu.VMEM((CHUNKS, NY, M, LANES, LANES), BF16),
            pltpu.VMEM((CHUNKS, NZ, R, LANES), F32),
            pltpu.VMEM((2, CHUNKS, 4, R, LANES), F32),
            pltpu.VMEM((CHUNKS, 2 * HALF, LANES), BF16),
            pltpu.VMEM((CHUNKS, 2 * HALF, LANES), BF16),
            pltpu.VMEM((2, CHUNKS, NY, R, LANES), F32),
            pltpu.VMEM((2, CHUNKS, 3, R, LANES), F32),
            pltpu.VMEM((CHUNKS, R, LANES), F32),
            pltpu.VMEM((CHUNKS, R, LANES), F32),
            pltpu.VMEM((CHUNKS, R, LANES), F32),
            pltpu.VMEM((CHUNKS, R, LANES), F32),
            pltpu.VMEM((2, CHUNKS, NY, 4, LANES), F32),
            pltpu.VMEM((2, CHUNKS, NZ, 4, LANES), F32),
            dma((1,)),
            dma((M,)),
            dma((2,)),
            dma((3, M)),
            dma((1,)),
            dma((4,)),
            dma((4, CHUNKS)),
            dma((4 * STAGES,)),
            dma((4 * STAGES,)),
        ],
        compiler_params=pltpu.CompilerParams(
            collective_id=0, has_side_effects=True, vmem_limit_bytes=56 * 1024 * 1024
        ),
    )(sub, weights)


def solution(mesh):
    torus = Mesh(mesh.devices.reshape(NY, NZ, NX, 2), ("y", "z", "x", "c"))
    spec = P(None, ("y", "z"), ("x", "c"))
    out = P(("y", "z"), ("x", "c"))
    return jax.shard_map(shards, mesh=torus, in_specs=(spec, spec), out_specs=(out, out), check_vma=False)
```

time: 168 us -> 146 us (0.87)
  Pallas kernels: 162 us -> 141 us
    pallas_call x1, Pallas kernels: 162 us -> 141 us  [shards(): pl.pallas_call(kernel, out_shape=(block, block), in_specs=[vmem, vmem], o...]
where the time goes in v2:
time: 146 us
  Pallas kernels  141 us (97%)
  local copies, waits for them, and re-layouts  4.96 us (3%)
    pallas_call x1, Pallas kernels, shards(): pl.pallas_call(kernel, out_shape=(block, block), in_specs=[vmem, vmem], o...  141 us
    unnamed x5, local copies, waits for them, and re-layouts  3.85 us

profile of v2, /device:TPU:8, one launch (start us, length us, event | category | flops | bytes accessed | tf_op | source)
XLA Modules:
  0.0 146.3 jit_solution(15466965005530118990)
XLA Ops:
  0.6 1.3 copy.4
  1.9 0.2 copy.5
  2.2 0.9 pad.4.g_ref
  3.0 140.7 %shard_map.41 = (f32[112,896]{1,0:T(8,128)}, f32[112,896]{1,0:T(8,128)}) custom-call(bf16[4,4,112,128]{3,2,1,0:T(8,128)(2,1)} %pad.4.g_ref, bf16[4,112,896]{2,1,0:T(8,128)(2,1)} %w_ref.1), custom_call_target="tpu_custom_call" | custom-call | tf_op jit(solution)/shard_map/pallas_call | solution.py:454
  143.7 0.0 copy-start
  143.7 1.8 %copy.8 = f32[112,896]{1,0:T(8,128)} copy(f32[112,896]{1,0:T(8,128)} %get-tuple-element.4) | data formatting | bytes 802816
  145.5 0.0 copy-done
  145.5 0.7 copy.9
Async XLA Ops:
  143.7 1.8 %copy-start = (f32[112,896]{1,0:T(8,128)S(1)}, f32[112,896]{1,0:T(8,128)}, u32[]{:S(2)}) copy-start(f32[112,896]{1,0:T(8,128)} %get-tuple-element.5) | copy-start | bytes 1204228
